TPU v7x, 32 devices: a whole 2x2x4 slice. The times are simulated.
32 devices in a mesh: row: 8 (over y, x, core), col: 4 (over z).
Axes of the slice: x: 2, y: 2, z: 4, core: 2. Of those that a mesh axis runs over, the one named last changes fastest.
Arguments:
- species: float32 [4, 64, 32, 256], P(None, None, 'row', 'col'), may hold values from -6 to 6
- symbol_x: float32 [64], replicated, may hold values from 0.3 to 3
- symbol_y: float32 [32], replicated, may hold values from 0.3 to 3
- symbol_z: float32 [256], replicated, may hold values from 0.3 to 3
Outputs:
- coefficients: float32 [4, 64, 32, 256], P(None, 'row', 'col')
All inputs are finite; a program needn't handle non-finite values.
Results may differ from a plain program's by a relative error of at most 0.00007.
Values sent between devices are 32-bit elements; how exact they have to be, the bound alone decides.
A program may use at most 64 MiB of HBM per device.

v0:
```python
import jax
import jax.numpy as jnp
from jax import lax
from jax.sharding import PartitionSpec as P


def transform_table(count):
    rank = jnp.arange(count)
    angle = (
        jnp.pi
        / (count + 1)
        * ((rank[:, None] + 1) * (rank[None, :] + 1) % (2 * count + 2)).astype(jnp.float32)
    )
    return jnp.sin(angle) * (2.0 / (count + 1)) ** 0.5


def transform_dim(values, dim):
    moved = jnp.tensordot(
        values,
        transform_table(values.shape[dim]),
        axes=([dim], [0]),
        precision=lax.Precision.HIGHEST,
    )
    return jnp.moveaxis(moved, -1, dim)


def on_device(species, symbol_x, symbol_y, symbol_z):
    part_values = species
    part_values = transform_dim(part_values, 1)
    part_values = lax.all_to_all(part_values, "row", split_axis=1, concat_axis=2, tiled=True)
    part_values = transform_dim(part_values, 2)
    block_values = part_values
    block_values = lax.all_to_all(block_values, "col", split_axis=2, concat_axis=3, tiled=True)
    block_values = transform_dim(block_values, 3)
    share_x = block_values.shape[1]
    part_x = lax.dynamic_slice_in_dim(symbol_x, lax.axis_index("row") * share_x, share_x)
    share_y = block_values.shape[2]
    part_y = lax.dynamic_slice_in_dim(symbol_y, lax.axis_index("col") * share_y, share_y)
    symbol = part_x[:, None, None] + part_y[None, :, None] + symbol_z[None, None, :]
    block_values = block_values / symbol
    return block_values


def solution(mesh):
    placed = (P(None, None, "row", "col"), P(), P(), P())
    return jax.shard_map(
        on_device,
        mesh=mesh,
        in_specs=placed,
        out_specs=P(None, "row", "col", None),
        check_vma=False,
    )
```

profile of v0, /device:TPU:0, one launch (start us, length us, event | category | flops | bytes accessed | tf_op | source)
XLA Modules:
  0.0 37.5 jit_solution(5117100488753793122)
XLA Ops:
  0.0 1.0 %copy-done = f32[4,64,4,64]{3,2,1,0:T(4,128)S(1)} copy-done((f32[4,64,4,64]{3,2,1,0:T(4,128)S(1)}, f32[4,64,4,64]{3,2,1,0:T(4,128)}, u32[]{:S(2)}) %copy-start) | copy-done | bytes 262168
  1.0 0.8 %convolution_bitcast_fusion.1 = f32[4,64,4,64]{3,1,2,0:T(8,128)S(1)} fusion(f32[4,64,4,64]{3,2,1,0:T(4,128)S(1)} %copy-done, s32[64]{0:T(128)S(1)} %iota_add_fusion.2), kind=kOutput, calls=%fused_computation.1 | convolution fusion | flops 50372608 | bytes 524544 | tf_op jit(solution)/shard_map/dot_general | solution.py:18
  1.8 0.3 copy.23
  2.2 1.2 %reshape.67 = f32[8,1,8192]{2,1,0:T(1,128)} reshape(f32[64,4,4,64]{3,2,1,0:T(4,128)S(1)} %bitcast.38) | data formatting | bytes 524288
  3.4 5.2 %all-to-all-start = ((f32[8,1,8192]{2,1,0:T(1,128)}), f32[8,1,8192]{2,1,0:T(1,128)S(1)}, u32[]{:S(2)}, u32[]{:S(2)}) async-start(f32[8,1,8192]{2,1,0:T(1,128)} %reshape.67), calls=%async_computation | async-start | bytes 524288 | tf_op jit(solution)/shard_map/all_to_all | solution.py:30
  8.6 0.7 %copy-done.2 = f32[32]{0:T(128)S(1)} copy-done((f32[32]{0:T(128)S(1)}, f32[32]{0:T(128)}, u32[]{:S(2)}) %copy-start.2) | copy-done | bytes 152
  9.2 0.1 dynamic_slice.7
  9.3 0.7 %copy-done.3 = f32[64]{0:T(128)S(1)} copy-done((f32[64]{0:T(128)S(1)}, f32[64]{0:T(128)}, u32[]{:S(2)}) %copy-start.3) | copy-done | bytes 280
  10.0 5.4 %all-to-all-done = f32[8,1,8192]{2,1,0:T(1,128)S(1)} async-done(((f32[8,1,8192]{2,1,0:T(1,128)}), f32[8,1,8192]{2,1,0:T(1,128)S(1)}, u32[]{:S(2)}, u32[]{:S(2)}) %all-to-all-start) | async-done | bytes 262176 | tf_op jit(solution)/shard_map/all_to_all | solution.py:30
  15.5 0.6 %broadcast.68 = f32[]{:T(128)} broadcast(f32[]{:T(128)} %constant.133), dimensions={} | broadcast | bytes 8 | tf_op jit(solution)/shard_map/all_to_all | solution.py:30
  16.0 1.2 %reduce = f32[8,8192]{1,0:T(8,128)S(1)} reduce(f32[8,1,8192]{2,1,0:T(1,128)S(1)} %all-to-all-done, f32[]{:T(128)} %broadcast.68), dimensions={1}, to_apply=%all_to_all.26.reduce_sub_computation | reduce | bytes 524292 | tf_op jit(solution)/shard_map/all_to_all | solution.py:30
  17.3 0.3 reshape.68
  17.6 0.1 copy.10
  17.8 0.7 %convolution_bitcast_fusion = f32[4,8,32,64]{3,2,1,0:T(8,128)S(1)} fusion(f32[4,8,32,64]{3,2,1,0:T(8,128)S(1)} %bitcast.37, s32[32]{0:T(128)S(1)} %iota_add_fusion.1), kind=kOutput, calls=%fused_computation | convolution fusion | flops 25176064 | bytes 524416 | tf_op jit(solution)/shard_map/dot_general | solution.py:18
  18.5 0.3 copy.22
  18.8 1.0 %reshape.69 = f32[4,1,16384]{2,1,0:T(1,128)} reshape(f32[32,4,8,64]{3,2,1,0:T(8,128)S(1)} %bitcast.40) | data formatting | bytes 524288
  19.8 4.9 %all-to-all-start.1 = ((f32[4,1,16384]{2,1,0:T(1,128)}), f32[4,1,16384]{2,1,0:T(1,128)S(1)}, u32[]{:S(2)}, u32[]{:S(2)}) async-start(f32[4,1,16384]{2,1,0:T(1,128)} %reshape.69), calls=%async_computation.1 | async-start | bytes 524288 | tf_op jit(solution)/shard_map/all_to_all | solution.py:33
  24.8 0.7 %copy-done.1 = f32[256]{0:T(256)S(1)} copy-done((f32[256]{0:T(256)S(1)}, f32[256]{0:T(256)}, u32[]{:S(2)}) %copy-start.1) | copy-done | bytes 1048
  25.5 7.5 %all-to-all-done.1 = f32[4,1,16384]{2,1,0:T(1,128)S(1)} async-done(((f32[4,1,16384]{2,1,0:T(1,128)}), f32[4,1,16384]{2,1,0:T(1,128)S(1)}, u32[]{:S(2)}, u32[]{:S(2)}) %all-to-all-start.1) | async-done | bytes 262176 | tf_op jit(solution)/shard_map/all_to_all | solution.py:33
  33.0 1.4 %reduce.1 = f32[4,16384]{1,0:T(4,128)S(1)} reduce(f32[4,1,16384]{2,1,0:T(1,128)S(1)} %all-to-all-done.1, f32[]{:T(128)} %broadcast.68), dimensions={1}, to_apply=%all_to_all.30.reduce_sub_computation | reduce | bytes 524292 | tf_op jit(solution)/shard_map/all_to_all | solution.py:33
  34.4 0.3 reshape.70
  34.7 0.3 copy.21
  35.0 0.3 all_to_all.33
  35.4 2.2 %convolution_divide_fusion = f32[4,8,8,256]{3,2,1,0:T(8,128)} fusion(f32[4,8,8,256]{3,2,1,0:T(8,128)S(1)} %all_to_all.33, f32[8,8,256]{2,1,0:T(8,128)S(1)} %broadcast_add_fusion, s32[256]{0:T(256)S(1)} %iota_add_fusion), kind=kOutput, calls=%fused_computation.2 | convolution fusion | flops 202047488 | bytes 590848 | tf_op jit(solution)/shard_map/dot_general | solution.py:18
  (10 shorter events, 0.2 us)
Async XLA Ops:
  0.0 1.0 %copy-start = (f32[4,64,4,64]{3,2,1,0:T(4,128)S(1)}, f32[4,64,4,64]{3,2,1,0:T(4,128)}, u32[]{:S(2)}) copy-start(f32[4,64,4,64]{3,2,1,0:T(4,128)} %param.4) | copy-start | bytes 786436
  3.4 12.1 %all-to-all-start = ((f32[8,1,8192]{2,1,0:T(1,128)}), f32[8,1,8192]{2,1,0:T(1,128)S(1)}, u32[]{:S(2)}, u32[]{:S(2)}) async-start(f32[8,1,8192]{2,1,0:T(1,128)} %reshape.67), calls=%async_computation | async-start | bytes 524288 | tf_op jit(solution)/shard_map/all_to_all | solution.py:30
  8.6 0.7 %copy-start.2 = (f32[32]{0:T(128)S(1)}, f32[32]{0:T(128)}, u32[]{:S(2)}) copy-start(f32[32]{0:T(128)} %param.6) | copy-start | bytes 388
  9.3 0.7 %copy-start.3 = (f32[64]{0:T(128)S(1)}, f32[64]{0:T(128)}, u32[]{:S(2)}) copy-start(f32[64]{0:T(128)} %param.5) | copy-start | bytes 772
  19.8 13.2 %all-to-all-start.1 = ((f32[4,1,16384]{2,1,0:T(1,128)}), f32[4,1,16384]{2,1,0:T(1,128)S(1)}, u32[]{:S(2)}, u32[]{:S(2)}) async-start(f32[4,1,16384]{2,1,0:T(1,128)} %reshape.69), calls=%async_computation.1 | async-start | bytes 524288 | tf_op jit(solution)/shard_map/all_to_all | solution.py:33
  24.8 0.7 %copy-start.1 = (f32[256]{0:T(256)S(1)}, f32[256]{0:T(256)}, u32[]{:S(2)}) copy-start(f32[256]{0:T(256)} %param.7) | copy-start | bytes 3076
where the time goes:
time: 37.9 us; the launch traced here: 37.5 us
  waiting for transfers between devices  12.9 us (34%)
  starting transfers between devices  10.1 us (27%)
  local copies, waits for them, and re-layouts  8.06 us (21%)
  matrix products  3.65 us (10%)
  other arithmetic  2.75 us (7%)
    all_to_all x1, waiting for transfers between devices, on_device(): lax.all_to_all(block_values, 'col', split_axis=2, concat_axis=3, tiled=True)  7.5 us
    unnamed x12, local copies, waits for them, and re-layouts  5.87 us
    all_to_all x1, waiting for transfers between devices, on_device(): lax.all_to_all(part_values, 'row', split_axis=1, concat_axis=2, tiled=True)  5.44 us
    all_to_all x1, starting transfers between devices, on_device(): lax.all_to_all(part_values, 'row', split_axis=1, concat_axis=2, tiled=True)  5.2 us
    all_to_all x1, starting transfers between devices, on_device(): lax.all_to_all(block_values, 'col', split_axis=2, concat_axis=3, tiled=True)  4.87 us
    dot_general x3, matrix products, transform_dim(): jnp.tensordot(values, transform_table(values.shape[dim]), axes=([dim], [0...  3.65 us
    all_to_all x1, other arithmetic, on_device(): lax.all_to_all(block_values, 'col', split_axis=2, concat_axis=3, tiled=True)  1.36 us
    all_to_all x1, other arithmetic, on_device(): lax.all_to_all(part_values, 'row', split_axis=1, concat_axis=2, tiled=True)  1.24 us
  transfers between devices with their start and end apart: 2, of which 2 were waited for; matrix products, arithmetic and copies ran while one was open for 1% of the time, Pallas kernels for 0%

commit v1 on v0

v1 whole, which is shorter than its diff:
```python
import functools

import jax
import jax.numpy as jnp
import ml_dtypes
import numpy as np
from jax import lax
from jax.experimental import pallas as pl
from jax.experimental.pallas import tpu as pltpu
from jax.sharding import PartitionSpec as P

MESH = pl.DeviceIdType.MESH
LANES = 128


def table(count):
    rank = np.arange(count, dtype=np.int64) + 1
    angle = np.pi / (count + 1) * ((rank[:, None] * rank[None, :]) % (2 * count + 2))
    return (np.sin(angle) * (2.0 / (count + 1)) ** 0.5).astype(np.float32)


def halves(values):
    high = values.astype(ml_dtypes.bfloat16)
    low = (values - high.astype(np.float32)).astype(ml_dtypes.bfloat16)
    return np.stack([high, low])


def split(values):
    high = values.astype(jnp.bfloat16)
    low = (values - high.astype(jnp.float32)).astype(jnp.bfloat16)
    return high, low


def dot(a, b):
    return jnp.dot(a, b, preferred_element_type=jnp.float32)


def left_dot(high, low, data):
    data_high, data_low = data
    return dot(high, data_high) + dot(high, data_low) + dot(low, data_high)


def partner(me, step, count):
    if count & (count - 1):
        return lax.rem(me + step, count)
    to, bit = me, 1
    while bit < count:
        if step & bit:
            to = to + bit * (1 - 2 * lax.rem(me // bit, 2))
        bit *= 2
    return to


def kernel(
    dims,
    species, symbol_x, symbol_y, symbol_z, table_x, table_y, table_z,
    out,
    space, mx, my, mz, sx, sy, sz, send_a, recv_a, send_b, recv_b, inverse,
    load_sem, a_send, a_recv, b_send, b_recv,
):
    fields, pack, rows, cols, cuts, xc, yb, zl = dims
    groups = fields // pack
    row, col = lax.axis_index("row"), lax.axis_index("col")

    loads = [
        pltpu.make_async_copy(src, dst, load_sem.at[i])
        for i, (src, dst) in enumerate([
            (species, space), (table_x, mx), (symbol_x, sx), (symbol_y, sy), (symbol_z, sz), (table_y, my), (table_z, mz),
        ])
    ]
    for load in loads:
        load.start()
    row_steps = list(range(rows - 1, 0, -1))
    col_steps = list(range(cols - 1, 0, -1))
    barrier = pltpu.get_barrier_semaphore()
    for step in col_steps:
        pl.semaphore_signal(barrier, inc=1, device_id={"col": partner(col, step, cols)}, device_id_type=MESH)
    for step in row_steps:
        pl.semaphore_signal(barrier, inc=1, device_id={"row": partner(row, step, rows)}, device_id_type=MESH)

    loads[0].wait()
    data = []
    for g in range(groups):
        packed = jnp.concatenate([space[g * pack + i] for i in range(pack)], axis=-1)
        data.append(split(packed))
    loads[1].wait()

    chunks = [(q, g) for q in range(cuts) for g in range(groups)]
    for i, (q, g) in enumerate(chunks):
        send_a[q, g] = left_dot(mx[0, q], mx[1, q], data[g]).reshape(send_a.shape[2:])
        if i == 0:
            pl.semaphore_wait(barrier, len(row_steps) + len(col_steps))
        for step in row_steps:
            to = partner(row, step, rows)
            pltpu.make_async_remote_copy(
                src_ref=send_a.at[q, g, to], dst_ref=recv_a.at[q, g, row],
                send_sem=a_send.at[i, step], recv_sem=a_recv.at[i, step],
                device_id={"row": to}, device_id_type=MESH,
            ).start()
        recv_a[q, g, row] = send_a[q, g, row]

    for load in loads[2:]:
        load.wait()
    part_y = jnp.zeros((yb, 1), jnp.float32)
    at = lax.broadcasted_iota(jnp.int32, (yb, 1), 0)
    for j in range(yb):
        part_y = jnp.where(at == j, sy[col * yb + j], part_y)
    for i in range(cuts * xc):
        inverse[i] = 1.0 / ((sx[row * (cuts * xc) + i] + part_y) + sz[...])

    for i, (q, g) in enumerate(chunks):
        for step in row_steps:
            to = partner(row, step, rows)
            pltpu.make_async_remote_copy(
                src_ref=send_a.at[q, g, to], dst_ref=recv_a.at[q, g, row],
                send_sem=a_send.at[i, step], recv_sem=a_recv.at[i, step],
                device_id={"row": to}, device_id_type=MESH,
            ).wait_recv()
        lines = recv_a[q, g].reshape(-1, LANES)
        send_b[q, g] = left_dot(my[0], my[1], split(lines)).reshape(send_b.shape[2:])
        for step in col_steps:
            to = partner(col, step, cols)
            pltpu.make_async_remote_copy(
                src_ref=send_b.at[q, g, to], dst_ref=recv_b.at[q, g, col],
                send_sem=b_send.at[i, step], recv_sem=b_recv.at[i, step],
                device_id={"col": to}, device_id_type=MESH,
            ).start()
        recv_b[q, g, col] = send_b[q, g, col]

    for i, (q, g) in enumerate(chunks):
        for step in col_steps:
            to = partner(col, step, cols)
            pltpu.make_async_remote_copy(
                src_ref=send_b.at[q, g, to], dst_ref=recv_b.at[q, g, col],
                send_sem=b_send.at[i, step], recv_sem=b_recv.at[i, step],
                device_id={"col": to}, device_id_type=MESH,
            ).wait_recv()
        blocks = [recv_b[q, g, c] for c in range(cols)]
        lines = jnp.concatenate(
            [jnp.concatenate([b[:, k * zl:(k + 1) * zl] for b in blocks], axis=-1) for k in range(pack)], axis=0
        )
        high, low = split(lines)
        result = dot(high, mz[0]) + dot(high, mz[1]) + dot(low, mz[0])
        factor = inverse[q * xc:(q + 1) * xc].reshape(xc * yb, -1)
        for k in range(pack):
            out[g * pack + k, q * xc * yb:(q + 1) * xc * yb] = result[k * xc * yb:(k + 1) * xc * yb] * factor

    for i, (q, g) in enumerate(chunks):
        for step in row_steps:
            to = partner(row, step, rows)
            pltpu.make_async_remote_copy(
                src_ref=send_a.at[q, g, to], dst_ref=recv_a.at[q, g, row],
                send_sem=a_send.at[i, step], recv_sem=a_recv.at[i, step],
                device_id={"row": to}, device_id_type=MESH,
            ).wait_send()
        for step in col_steps:
            to = partner(col, step, cols)
            pltpu.make_async_remote_copy(
                src_ref=send_b.at[q, g, to], dst_ref=recv_b.at[q, g, col],
                send_sem=b_send.at[i, step], recv_sem=b_recv.at[i, step],
                device_id={"col": to}, device_id_type=MESH,
            ).wait_send()


def on_device(rows, cols, species, symbol_x, symbol_y, symbol_z):
    fields, x, yl, zl = species.shape
    y, z = symbol_y.shape[0], symbol_z.shape[0]
    xb, yb = x // rows, y // cols
    pack = LANES // zl
    groups = fields // pack
    cuts = 2
    xc = xb // cuts

    hx = table(x)
    eye = np.eye(yl, dtype=np.float32)
    full_x = np.einsum("rqia,yb->qriyab", hx.T.reshape(rows, cuts, xc, x), eye).reshape(cuts, rows * xc * yl, x * yl)
    hy = table(y).T.reshape(cols, yb, rows, yl)
    full_y = np.einsum("cmry,ij->cimrjy", hy, np.eye(xc, dtype=np.float32)).reshape(cols * xc * yb, rows * xc * yl)
    tables = [halves(full_x), halves(full_y), halves(table(z))]

    any_space = pl.BlockSpec(memory_space=pltpu.MemorySpace.HBM)
    chunks = cuts * groups
    a_shape = (cuts, groups, rows, xc * yl, LANES)
    b_shape = (cuts, groups, cols, xc * yb, LANES)
    dma = pltpu.SemaphoreType.DMA
    out = pl.pallas_call(
        functools.partial(kernel, (fields, pack, rows, cols, cuts, xc, yb, zl)),
        out_shape=jax.ShapeDtypeStruct((fields, xb * yb, z), jnp.float32),
        in_specs=[any_space] * 7,
        out_specs=pl.BlockSpec(memory_space=pltpu.MemorySpace.VMEM),
        scratch_shapes=[
            pltpu.VMEM((fields, x * yl, zl), jnp.float32),
            pltpu.VMEM(tables[0].shape, jnp.bfloat16),
            pltpu.VMEM(tables[1].shape, jnp.bfloat16),
            pltpu.VMEM(tables[2].shape, jnp.bfloat16),
            pltpu.SMEM((x,), jnp.float32),
            pltpu.SMEM((y,), jnp.float32),
            pltpu.VMEM((1, z), jnp.float32),
            pltpu.VMEM(a_shape, jnp.float32),
            pltpu.VMEM(a_shape, jnp.float32),
            pltpu.VMEM(b_shape, jnp.float32),
            pltpu.VMEM(b_shape, jnp.float32),
            pltpu.VMEM((xb, yb, z), jnp.float32),
            dma((7,)),
            dma((chunks, rows)),
            dma((chunks, rows)),
            dma((chunks, cols)),
            dma((chunks, cols)),
        ],
        compiler_params=pltpu.CompilerParams(
            collective_id=0, has_side_effects=True, vmem_limit_bytes=60 * 1024 * 1024
        ),
    )(
        species.reshape(fields, x * yl, zl), symbol_x, symbol_y, symbol_z.reshape(1, z),
        *[jnp.asarray(t) for t in tables],
    )
    return out.reshape(fields, xb, yb, z)


def solution(mesh):
    placed = (P(None, None, "row", "col"), P(), P(), P())
    return jax.shard_map(
        functools.partial(on_device, mesh.shape["row"], mesh.shape["col"]),
        mesh=mesh,
        in_specs=placed,
        out_specs=P(None, "row", "col", None),
        check_vma=False,
    )
```

time: 37.9 us -> 20.4 us (0.54)
  Pallas kernels: 0 us -> 18.5 us
  waiting for transfers between devices: 12.9 us -> 0 us
  starting transfers between devices: 10.1 us -> 0 us
  local copies, waits for them, and re-layouts: 8.06 us -> 1.67 us
  matrix products: 3.65 us -> 0 us
  other arithmetic: 2.75 us -> 0 us
    pallas_call x0 -> x1, Pallas kernels: none -> 18.5 us  [on_device(): pl.pallas_call(functools.partial(kernel, (fields, pack, rows, cols, cuts,...]
    all_to_all x2 -> x0, waiting for transfers between devices: 12.9 us -> none  [the longest x1 7.5 us: on_device(): lax.all_to_all(block_values, 'col', split_axis=2, concat_axis=3, tiled=True)]
    all_to_all x2 -> x0, starting transfers between devices: 10.1 us -> none  [the longest x1 5.2 us: on_device(): lax.all_to_all(part_values, 'row', split_axis=1, concat_axis=2, tiled=True)]
    unnamed x12 -> x1, local copies, waits for them, and re-layouts: 5.87 us -> 1.67 us
    dot_general x3 -> x0, matrix products: 3.65 us -> none  [transform_dim(): jnp.tensordot(values, transform_table(values.shape[dim]), axes=([dim], [0...]
    all_to_all x2 -> x0, other arithmetic: 2.6 us -> none  [the longest x1 1.36 us: on_device(): lax.all_to_all(block_values, 'col', split_axis=2, concat_axis=3, tiled=True)]
    all_to_all x4 -> x0, local copies, waits for them, and re-layouts: 1.39 us -> none  [the longest x2 0.71 us: on_device(): lax.all_to_all(part_values, 'row', split_axis=1, concat_axis=2, tiled=True)]
    transpose x2 -> x0, local copies, waits for them, and re-layouts: 0.65 us -> none  [transform_dim(): return jnp.moveaxis(moved, -1, dim)]
  transfers between devices with their start and end apart: 2 -> 0, of which waited for: 2 -> 0; matrix products, arithmetic and copies ran while one was open for 1% -> 0% of each run, Pallas kernels for 0% -> 0%
where the time goes in v1:
time: 20.4 us; the launch traced here: 20.2 us
  Pallas kernels  18.5 us (91%)
  local copies, waits for them, and re-layouts  1.67 us (8%)
    pallas_call x1, Pallas kernels, on_device(): pl.pallas_call(functools.partial(kernel, (fields, pack, rows, cols, cuts,...  18.5 us
    unnamed x1, local copies, waits for them, and re-layouts  1.67 us

profile of v1, /device:TPU:0, one launch (start us, length us, event | category | flops | bytes accessed | tf_op | source)
XLA Modules:
  0.0 20.2 jit_solution(15961345283982354946)
XLA Ops:
  0.0 18.5 %shard_map.73 = f32[4,64,256]{2,1,0:T(8,128)} custom-call(f32[4,256,64]{2,1,0:T(8,128)} %bitcast.4, f32[64]{0:T(128)} %symbol_x.1, f32[32]{0:T(128)} %symbol_y.1, f32[1,256]{1,0:T(1,128)} %bitcast.5, bf16[2,2,128,256]{3,2,1,0:T(8,128)(2,1)} %constant.6.clone.table_x, bf16[2,128,128]{2,1,0:T(8,128)(2,1)} %constant.7.clone.table_y, ...), custom_call_target="tpu_custom_call" | custom-call | tf_op jit(solution)/shard_map/pallas_call | solution.py:186
  18.5 1.7 %copy.9 = f32[4,8,8,256]{3,2,1,0:T(8,128)} copy(f32[4,8,8,256]{3,2,1,0:T(8,128)} %bitcast.3) | data formatting | bytes 524288

commit v2 on v1

v2 whole, which is shorter than its diff:
```python
import functools

import jax
import jax.numpy as jnp
import ml_dtypes
import numpy as np
from jax import lax
from jax.experimental import pallas as pl
from jax.experimental.pallas import tpu as pltpu
from jax.sharding import PartitionSpec as P

MESH = pl.DeviceIdType.MESH
LANES = 128


def table(count):
    rank = np.arange(count, dtype=np.int64) + 1
    angle = np.pi / (count + 1) * ((rank[:, None] * rank[None, :]) % (2 * count + 2))
    return (np.sin(angle) * (2.0 / (count + 1)) ** 0.5).astype(np.float32)


def halves(values):
    high = values.astype(ml_dtypes.bfloat16)
    low = (values - high.astype(np.float32)).astype(ml_dtypes.bfloat16)
    return np.stack([high, low])


def split(values):
    high = values.astype(jnp.bfloat16)
    low = (values - high.astype(jnp.float32)).astype(jnp.bfloat16)
    return high, low


def side_by_side(values):
    return jnp.concatenate(split(values), axis=-1)


def dot(a, b):
    return jnp.dot(a, b, preferred_element_type=jnp.float32)


def left_dot(both, data):
    count, width = both.shape[0] // 2, data.shape[-1] // 2
    terms = dot(both, data)
    sides = terms[:, :width] + terms[:, width:]
    return sides[:count] + sides[count:]


def batches(count):
    return [[i] for i in range(count - 2)] + [[count - 2, count - 1]]


def partner(me, step, count):
    if count & (count - 1):
        return lax.rem(me + step, count)
    to, bit = me, 1
    while bit < count:
        if step & bit:
            to = to + bit * (1 - 2 * lax.rem(me // bit, 2))
        bit *= 2
    return to


def kernel(
    dims,
    species, symbol_x, symbol_y, symbol_z, table_x, table_y, table_z,
    out,
    space, mx, my, mz, sx, sy, sz, send_a, recv_a, send_b, recv_b, inverse, held,
    load_sem, store_sem, a_send, a_recv, b_send, b_recv,
):
    fields, pack, rows, cols, cuts, xc, yb, zl = dims
    groups = fields // pack
    row, col = lax.axis_index("row"), lax.axis_index("col")

    pieces = [(species.at[f], space.at[f]) for f in range(fields)]
    pieces += [(table_x.at[q], mx.at[q]) for q in range(cuts)]
    pieces += [(symbol_x, sx), (symbol_y, sy), (symbol_z, sz), (table_y, my), (table_z, mz)]
    loads = [pltpu.make_async_copy(src, dst, load_sem.at[i]) for i, (src, dst) in enumerate(pieces)]
    urgent = list(range(pack)) + [fields]
    for i in urgent:
        loads[i].start()
    row_steps = list(range(rows - 1, 0, -1))
    col_steps = list(range(cols - 1, 0, -1))
    barrier = pltpu.get_barrier_semaphore()
    for step in col_steps:
        pl.semaphore_signal(barrier, inc=1, device_id={"col": partner(col, step, cols)}, device_id_type=MESH)
    for step in row_steps:
        pl.semaphore_signal(barrier, inc=1, device_id={"row": partner(row, step, rows)}, device_id_type=MESH)
    for i in range(fields + cuts):
        if i not in urgent:
            loads[i].start()

    chunks = [(q, g) for g in range(groups) for q in range(cuts)]
    for i, (q, g) in enumerate(chunks):
        if q == 0:
            for k in range(pack):
                loads[g * pack + k].wait()
            data = side_by_side(jnp.concatenate([space[g * pack + k] for k in range(pack)], axis=-1))
        if g == 0:
            loads[fields + q].wait()
        send_a[q, g] = left_dot(mx[q], data).reshape(send_a.shape[2:])
        if i == 0:
            for load in loads[fields + cuts:]:
                load.start()
            pl.semaphore_wait(barrier, len(row_steps) + len(col_steps))
        for step in row_steps:
            to = partner(row, step, rows)
            pltpu.make_async_remote_copy(
                src_ref=send_a.at[q, g, to], dst_ref=recv_a.at[q, g, row],
                send_sem=a_send, recv_sem=a_recv.at[i],
                device_id={"row": to}, device_id_type=MESH,
            ).start()
        recv_a[q, g, row] = send_a[q, g, row]

    for load in loads[fields + cuts:]:
        load.wait()
    part_y = jnp.zeros((yb, 1), jnp.float32)
    at = lax.broadcasted_iota(jnp.int32, (yb, 1), 0)
    for j in range(yb):
        part_y = jnp.where(at == j, sy[col * yb + j], part_y)
    for i in range(cuts * xc):
        inverse[i] = 1.0 / ((sx[row * (cuts * xc) + i] + part_y) + sz[...])

    for i, (q, g) in enumerate(chunks):
        arrived = recv_a.at[q, g, pl.ds(0, rows - 1)]
        pltpu.make_async_copy(arrived, arrived, a_recv.at[i]).wait()
        lines = recv_a[q, g].reshape(-1, LANES)
        send_b[q, g] = left_dot(my[...], side_by_side(lines)).reshape(send_b.shape[2:])
        for step in col_steps:
            to = partner(col, step, cols)
            pltpu.make_async_remote_copy(
                src_ref=send_b.at[q, g, to], dst_ref=recv_b.at[q, g, col],
                send_sem=b_send, recv_sem=b_recv.at[i],
                device_id={"col": to}, device_id_type=MESH,
            ).start()
        recv_b[q, g, col] = send_b[q, g, col]

    stores = []
    height = xc * yb
    for batch in batches(len(chunks)):
        lines = []
        for i in batch:
            q, g = chunks[i]
            arrived = recv_b.at[q, g, pl.ds(0, cols - 1)]
            pltpu.make_async_copy(arrived, arrived, b_recv.at[i]).wait()
            blocks = [recv_b[q, g, c] for c in range(cols)]
            for k in range(pack):
                lines.append(jnp.concatenate([b[:, k * zl:(k + 1) * zl] for b in blocks], axis=-1))
        high, low = split(jnp.concatenate(lines, axis=0))
        most = dot(jnp.concatenate([high, low], axis=0), mz[0])
        count = high.shape[0]
        result = most[:count] + most[count:] + dot(high, mz[1])
        for n, i in enumerate(batch):
            q, g = chunks[i]
            factor = inverse[q * xc:(q + 1) * xc].reshape(height, -1)
            for k in range(pack):
                at_line = (n * pack + k) * height
                held[i, k] = result[at_line:at_line + height] * factor
            stores.append(pltpu.make_async_copy(
                held.at[i], out.at[pl.ds(g * pack, pack), pl.ds(q * height, height)], store_sem.at[i]
            ))
            stores[-1].start()

    sent = send_a.at[:, :, pl.ds(0, rows - 1)]
    pltpu.make_async_copy(sent, sent, a_send).wait()
    sent = send_b.at[:, :, pl.ds(0, cols - 1)]
    pltpu.make_async_copy(sent, sent, b_send).wait()
    for store in stores:
        store.wait()


def on_device(rows, cols, species, symbol_x, symbol_y, symbol_z):
    fields, x, yl, zl = species.shape
    y, z = symbol_y.shape[0], symbol_z.shape[0]
    xb, yb = x // rows, y // cols
    pack = LANES // zl
    groups = fields // pack
    cuts = 2
    xc = xb // cuts

    hx = table(x)
    eye = np.eye(yl, dtype=np.float32)
    full_x = np.einsum("rqia,yb->qriyab", hx.T.reshape(rows, cuts, xc, x), eye).reshape(cuts, rows * xc * yl, x * yl)
    hy = table(y).T.reshape(cols, yb, rows, yl)
    full_y = np.einsum("cmry,ij->cimrjy", hy, np.eye(xc, dtype=np.float32)).reshape(cols * xc * yb, rows * xc * yl)
    tables = [
        np.concatenate(list(halves(full_x)), axis=1), np.concatenate(list(halves(full_y)), axis=0), halves(table(z))
    ]

    any_space = pl.BlockSpec(memory_space=pltpu.MemorySpace.HBM)
    chunks = cuts * groups
    a_shape = (cuts, groups, rows, xc * yl, LANES)
    b_shape = (cuts, groups, cols, xc * yb, LANES)
    dma = pltpu.SemaphoreType.DMA
    out = pl.pallas_call(
        functools.partial(kernel, (fields, pack, rows, cols, cuts, xc, yb, zl)),
        out_shape=pltpu.MemorySpace.VMEM((fields, xb * yb, z), jnp.float32),
        in_specs=[any_space] * 7,
        out_specs=pl.BlockSpec(memory_space=pl.ANY),
        scratch_shapes=[
            pltpu.VMEM((fields, x * yl, zl), jnp.float32),
            pltpu.VMEM(tables[0].shape, jnp.bfloat16),
            pltpu.VMEM(tables[1].shape, jnp.bfloat16),
            pltpu.VMEM(tables[2].shape, jnp.bfloat16),
            pltpu.SMEM((x,), jnp.float32),
            pltpu.SMEM((y,), jnp.float32),
            pltpu.VMEM((1, z), jnp.float32),
            pltpu.VMEM(a_shape, jnp.float32),
            pltpu.VMEM(a_shape, jnp.float32),
            pltpu.VMEM(b_shape, jnp.float32),
            pltpu.VMEM(b_shape, jnp.float32),
            pltpu.VMEM((xb, yb, z), jnp.float32),
            pltpu.VMEM((chunks, pack, xc * yb, z), jnp.float32),
            dma((fields + cuts + 5,)),
            dma((chunks,)),
            dma,
            dma((chunks,)),
            dma,
            dma((chunks,)),
        ],
        compiler_params=pltpu.CompilerParams(
            collective_id=0, has_side_effects=True, vmem_limit_bytes=60 * 1024 * 1024
        ),
    )(
        species.reshape(fields, x * yl, zl), symbol_x, symbol_y, symbol_z.reshape(1, z),
        *[jnp.asarray(t) for t in tables],
    )
    return out.reshape(fields, xb, yb, z)


def solution(mesh):
    placed = (P(None, None, "row", "col"), P(), P(), P())
    return jax.shard_map(
        functools.partial(on_device, mesh.shape["row"], mesh.shape["col"]),
        mesh=mesh,
        in_specs=placed,
        out_specs=P(None, "row", "col", None),
        check_vma=False,
    )
```

time: 20.4 us -> 17.9 us (0.88)
  Pallas kernels: 18.5 us -> 17.1 us
  local copies, waits for them, and re-layouts: 1.67 us -> 0.71 us
    pallas_call x1, Pallas kernels: 18.5 us -> 17.1 us  [on_device(): pl.pallas_call(functools.partial(kernel, (fields, pack, rows, cols, cuts,...]
    unnamed x1, local copies, waits for them, and re-layouts: 1.67 us -> 0.71 us
where the time goes in v2:
time: 17.9 us; the launch traced here: 17.8 us
  Pallas kernels  17.1 us (96%)
  local copies, waits for them, and re-layouts  0.71 us (4%)
    pallas_call x1, Pallas kernels, on_device(): pl.pallas_call(functools.partial(kernel, (fields, pack, rows, cols, cuts,...  17.1 us
    unnamed x1, local copies, waits for them, and re-layouts  0.71 us

profile of v2, /device:TPU:0, one launch (start us, length us, event | category | flops | bytes accessed | tf_op | source)
XLA Modules:
  0.0 17.8 jit_solution(17951578364295956758)
XLA Ops:
  0.0 17.1 %shard_map.73 = f32[4,64,256]{2,1,0:T(8,128)S(1)} custom-call(f32[4,256,64]{2,1,0:T(8,128)} %bitcast.4, f32[64]{0:T(128)} %symbol_x.1, f32[32]{0:T(128)} %symbol_y.1, f32[1,256]{1,0:T(1,128)} %bitcast.5, bf16[2,256,256]{2,1,0:T(8,128)(2,1)} %constant.6.clone.table_x, bf16[256,128]{1,0:T(8,128)(2,1)} %constant.7.clone.table_y, ...), custom_call_target="tpu_custom_call" | custom-call | tf_op jit(solution)/shard_map/pallas_call | solution.py:195
  17.1 0.7 %copy.9 = f32[4,8,8,256]{3,2,1,0:T(8,128)} copy(f32[4,8,8,256]{3,2,1,0:T(8,128)S(1)} %bitcast.3) | data formatting | bytes 524288

commit v3 on v2

--- a/solution.py
+++ b/solution.py
@@ -44,6 +44,14 @@
     terms = dot(both, data)
     sides = terms[:, :width] + terms[:, width:]
     return sides[:count] + sides[count:]
+
+
+def far_first(me, slot, count):
+    if count != 4:
+        return partner(me, count - 1 - slot, count)
+    inner = lax.rem((me + 1) // 2, 2)
+    outer_to, inner_to = (partner(me, step, count) for step in ((3, 2), (2, 3), (1, 1))[slot])
+    return outer_to + (inner_to - outer_to) * inner
 
 
 def batches(count):
@@ -121,20 +129,26 @@
     for i in range(cuts * xc):
         inverse[i] = 1.0 / ((sx[row * (cuts * xc) + i] + part_y) + sz[...])
 
+    def pass_on(i, slot):
+        q, g = chunks[i]
+        to = far_first(col, slot, cols)
+        pltpu.make_async_remote_copy(
+            src_ref=send_b.at[q, g, to], dst_ref=recv_b.at[q, g, col],
+            send_sem=b_send, recv_sem=b_recv.at[i],
+            device_id={"col": to}, device_id_type=MESH,
+        ).start()
+
     for i, (q, g) in enumerate(chunks):
         arrived = recv_a.at[q, g, pl.ds(0, rows - 1)]
         pltpu.make_async_copy(arrived, arrived, a_recv.at[i]).wait()
         lines = recv_a[q, g].reshape(-1, LANES)
         send_b[q, g] = left_dot(my[...], side_by_side(lines)).reshape(send_b.shape[2:])
-        for step in col_steps:
-            to = partner(col, step, cols)
-            pltpu.make_async_remote_copy(
-                src_ref=send_b.at[q, g, to], dst_ref=recv_b.at[q, g, col],
-                send_sem=b_send, recv_sem=b_recv.at[i],
-                device_id={"col": to}, device_id_type=MESH,
-            ).start()
+        for slot in range(1):
+            pass_on(i, slot)
         recv_b[q, g, col] = send_b[q, g, col]
 
+    for i, slot in [(i, s) for s in range(1, cols - 1) for i in range(len(chunks)) ]:
+        pass_on(i, slot)
     stores = []
     height = xc * yb
     for batch in batches(len(chunks)):

time: 17.9 us -> 17.3 us (0.966)
  Pallas kernels: 17.1 us -> 16.4 us
    pallas_call x1, Pallas kernels: 17.1 us -> 16.4 us  [on_device(): pl.pallas_call(functools.partial(kernel, (fields, pack, rows, cols, cuts,...]
where the time goes in v3:
time: 17.3 us; the launch traced here: 17.2 us
  Pallas kernels  16.4 us (95%)
  local copies, waits for them, and re-layouts  0.71 us (4%)
    pallas_call x1, Pallas kernels, on_device(): pl.pallas_call(functools.partial(kernel, (fields, pack, rows, cols, cuts,...  16.4 us
    unnamed x1, local copies, waits for them, and re-layouts  0.71 us

profile of v3, /device:TPU:0, one launch (start us, length us, event | category | flops | bytes accessed | tf_op | source)
XLA Modules:
  0.0 17.2 jit_solution(14539923154672672282)
XLA Ops:
  0.0 16.4 %shard_map.73 = f32[4,64,256]{2,1,0:T(8,128)S(1)} custom-call(f32[4,256,64]{2,1,0:T(8,128)} %bitcast.4, f32[64]{0:T(128)} %symbol_x.1, f32[32]{0:T(128)} %symbol_y.1, f32[1,256]{1,0:T(1,128)} %bitcast.5, bf16[2,256,256]{2,1,0:T(8,128)(2,1)} %constant.6.clone.table_x, bf16[256,128]{1,0:T(8,128)(2,1)} %constant.7.clone.table_y, ...), custom_call_target="tpu_custom_call" | custom-call | tf_op jit(solution)/shard_map/pallas_call | solution.py:209
  16.4 0.7 %copy.9 = f32[4,8,8,256]{3,2,1,0:T(8,128)} copy(f32[4,8,8,256]{3,2,1,0:T(8,128)S(1)} %bitcast.3) | data formatting | bytes 524288
